TPU v7x, 32 devices: a whole 2x2x4 slice. The times are simulated.
32 devices in a mesh: section: 16 (over z, y, core), tensor: 2 (over x).
Axes of the slice: x: 2, y: 2, z: 4, core: 2. Of those that a mesh axis runs over, the one named last changes fastest.
Arguments:
- saved: bfloat16 [16, 16, 64, 8192], P('section', None, 'tensor'), may hold values from -6 to 6
- offsets: int32 [16, 16], P('section'), may hold values from 0 to 15, as said below
Outputs:
- restored: float32 [16, 16, 64, 8192], P('section', None, None, 'tensor')
- block_sums: float32 [16, 16, 8192], P('section', None, 'tensor')
Inputs may be any that keep to these rules, and one draw needn't show every extreme that they name: Each row of offsets is a permutation of 0 to 15.
All inputs are finite; a program needn't handle non-finite values.
Results may differ from a plain program's by a relative error of at most 0.0003.
Values may be sent and summed in bfloat16 or wider, within the bound.
No kernel may reach another device: no remote copies, remote signals or barrier semaphores. Data moves between devices by JAX's collectives and lax.ppermute only.
A program may use at most 128 MiB of HBM per device.

v0:
```python
import jax
import jax.numpy as jnp
from jax import lax
from jax.sharding import PartitionSpec as P


def invert(table, count):
    return jnp.zeros((count,), jnp.int32).at[table].set(jnp.arange(count, dtype=jnp.int32))


def body(saved, offsets):
    count = lax.axis_size("section")
    mine = lax.axis_index("section")
    table = offsets[0]
    blocks = saved[0]
    order = invert((mine + table) % count, count)
    outgoing = jnp.take(blocks, order, axis=0)
    split_cols = lax.all_to_all(outgoing, "tensor", split_axis=2, concat_axis=1, tiled=True)
    arrived = lax.all_to_all(split_cols, "section", split_axis=0, concat_axis=0, tiled=True)
    restored = arrived.astype(jnp.float32)
    block_sums = jnp.sum(restored, axis=1)
    return (restored[None], block_sums[None])


def solution(mesh):
    return jax.shard_map(
        body,
        mesh=mesh,
        in_specs=(P("section", None, "tensor", None), P("section", None)),
        out_specs=(P("section", None, None, "tensor"), P("section", None, "tensor")),
        check_vma=False,
    )
```

profile of v0, /device:TPU:1, one launch (start us, length us, event | category | flops | bytes accessed | tf_op | source)
XLA Modules:
  0.0 462.9 jit_solution(6065663858853515315)
XLA Ops:
  0.6 0.7 fusion.1
  1.3 0.6 scatter_custom_fusion
  2.0 8.3 %gather_fusion = bf16[16,32,8192]{2,1,0:T(8,128)(2,1)} fusion(bf16[16,32,8192]{2,1,0:T(8,128)(2,1)} %bitcast.18, s32[1024]{0:T(1024)S(1)} %pad_clamp_fusion), kind=kCustom, calls=%fused_computation | custom fusion | bytes 16777280 | tf_op jit(solution)/shard_map/jit(_take)/gather | solution.py:17
  10.3 7.6 %broadcast_select_fusion = bf16[16,32,8192]{2,1,0:T(8,128)(2,1)} fusion(bf16[16,32,8192]{2,1,0:T(8,128)(2,1)} %gather_fusion, pred[16]{0:T(512)(128)(4,1)S(1)} %compare_and_fusion), kind=kLoop, calls=%fused_computation.4 | loop fusion | flops 4194304 | bytes 16777232 | tf_op jit(solution)/shard_map/jit(_take)/select_n | solution.py:17
  17.9 34.7 %copy.6 = bf16[16,32,8192]{1,0,2:T(8,128)(2,1)} copy(bf16[16,32,8192]{2,1,0:T(8,128)(2,1)} %broadcast_select_fusion) | data formatting | bytes 16777216 | tf_op jit(solution)/shard_map/jit(_take)/select_n | solution.py:17
  52.6 27.6 %reshape.82 = bf16[2,2,1048576]{2,1,0:T(2,128)(2,1)} reshape(bf16[8192,16,32]{2,1,0:T(8,128)(2,1)} %bitcast.15) | data formatting | bytes 16777216
  80.2 103.8 %all_to_all.23 = bf16[2,2,1048576]{2,1,0:T(2,128)(2,1)} all-to-all(bf16[2,2,1048576]{2,1,0:T(2,128)(2,1)} %reshape.82), channel_id=1, replica_groups=mesh['section'=16,'tensor'=2] {'tensor'}, dimensions={0} | all-to-all | bytes 16777216 | tf_op jit(solution)/shard_map/all_to_all | solution.py:18
  184.0 38.0 %reshape.83 = bf16[8192,16,32]{2,1,0:T(8,128)(2,1)} reshape(bf16[2,2,1048576]{2,1,0:T(2,128)(2,1)} %all_to_all.23) | data formatting | bytes 16777216
  222.0 33.7 %copy.7 = bf16[16,2,32,4096]{3,2,1,0:T(8,128)(2,1)} copy(bf16[16,2,32,4096]{2,0,3,1:T(8,128)(2,1)} %bitcast.16) | data formatting | bytes 16777216 | tf_op jit(solution)/shard_map/all_to_all | solution.py:18
  255.8 189.7 %all_to_all.24 = bf16[16,64,4096]{2,1,0:T(8,128)(2,1)S(1)} all-to-all(bf16[16,64,4096]{2,1,0:T(8,128)(2,1)} %bitcast.17), channel_id=1, replica_groups=mesh['section'=16,'tensor'=2] {'section'}, dimensions={0} | all-to-all | bytes 16777216 | tf_op jit(solution)/shard_map/all_to_all | solution.py:19
  445.4 0.0 copy-start
  445.5 3.2 copy-done
  448.7 2.4 convert_reduce_fusion
  451.1 11.8 %convert_bitcast_fusion = f32[1,16,64,4096]{3,2,1,0:T(8,128)} fusion(bf16[16,64,4096]{2,1,0:T(8,128)(2,1)} %copy-done), kind=kLoop, calls=%fused_computation.3 | loop fusion | flops 4194304 | bytes 25165824 | tf_op jit(solution)/shard_map/broadcast_in_dim | solution.py:22
  (4 shorter events, 0.0 us)
Async XLA Ops:
  445.4 3.2 copy-start
where the time goes:
time: 465 us; the launch traced here: 463 us
  blocking collectives  294 us (63%)
  local copies, waits for them, and re-layouts  146 us (31%)
  other arithmetic  22.6 us (5%)
    all_to_all x1, blocking collectives, body(): lax.all_to_all(split_cols, 'section', split_axis=0, concat_axis=0, tiled=...  190 us
    all_to_all x1, blocking collectives, body(): lax.all_to_all(outgoing, 'tensor', split_axis=2, concat_axis=1, tiled=True)  104 us
    unnamed x4, local copies, waits for them, and re-layouts  68.8 us
    select_n x1, local copies, waits for them, and re-layouts, body(): outgoing = jnp.take(blocks, order, axis=0)  34.7 us
    all_to_all x1, local copies, waits for them, and re-layouts, body(): lax.all_to_all(outgoing, 'tensor', split_axis=2, concat_axis=1, tiled=True)  33.7 us
    broadcast_in_dim x1, other arithmetic, body(): return (restored[None], block_sums[None])  11.8 us

commit v1 on v0

v1 whole, which is shorter than its diff:
```python
import jax
import jax.numpy as jnp
from jax import lax
from jax.experimental import pallas as pl
from jax.experimental.pallas import tpu as pltpu
from jax.sharding import PartitionSpec as P


def pack(blocks, target, parts):
    count, rows, cols = blocks.shape
    width = cols // parts

    def kernel(target_ref, in_ref, out_ref):
        for c in range(parts):
            out_ref[0, c] = in_ref[0, :, c * width:(c + 1) * width]

    return pl.pallas_call(
        kernel,
        grid_spec=pltpu.PrefetchScalarGridSpec(
            num_scalar_prefetch=1,
            grid=(count,),
            in_specs=[pl.BlockSpec((1, rows, cols), lambda j, target: (j, 0, 0))],
            out_specs=pl.BlockSpec((1, parts, rows, width), lambda j, target: (target[j], 0, 0, 0)),
        ),
        out_shape=jax.ShapeDtypeStruct((count, parts, rows, width), blocks.dtype),
        name="pack",
    )(target, blocks)


def unpack(arrived):
    count, rows, width = arrived.shape

    def kernel(in_ref, out_ref, sums_ref):
        s = pl.program_id(0)
        block = in_ref[0].astype(jnp.float32)
        out_ref[0, 0] = block
        sums_ref[0, pl.ds(s, 1), :] = jnp.sum(block, axis=0, keepdims=True)

    return pl.pallas_call(
        kernel,
        grid=(count,),
        in_specs=[pl.BlockSpec((1, rows, width), lambda s: (s, 0, 0))],
        out_specs=[
            pl.BlockSpec((1, 1, rows, width), lambda s: (0, s, 0, 0)),
            pl.BlockSpec((1, count, width), lambda s: (0, 0, 0)),
        ],
        out_shape=[
            jax.ShapeDtypeStruct((1, count, rows, width), jnp.float32),
            jax.ShapeDtypeStruct((1, count, width), jnp.float32),
        ],
        name="unpack",
    )(arrived)


def body(saved, offsets):
    count = lax.axis_size("section")
    parts = lax.axis_size("tensor")
    mine = lax.axis_index("section")
    _, _, rows, cols = saved.shape
    target = (mine + offsets[0]) % count
    outgoing = pack(saved[0], target, parts).reshape(count * parts, rows, cols // parts)
    arrived = lax.all_to_all(outgoing, ("section", "tensor"), split_axis=0, concat_axis=0, tiled=True)
    restored, block_sums = unpack(arrived.reshape(count, parts * rows, cols // parts))
    return (restored, block_sums)


def solution(mesh):
    return jax.shard_map(
        body,
        mesh=mesh,
        in_specs=(P("section", None, "tensor", None), P("section", None)),
        out_specs=(P("section", None, None, "tensor"), P("section", None, "tensor")),
        check_vma=False,
    )
```

time: 465 us -> 220 us (0.47)
  local copies, waits for them, and re-layouts: 146 us -> 0 us
  blocking collectives: 294 us -> 191 us
  Pallas kernels: 0 us -> 26.2 us
  other arithmetic: 22.6 us -> 1.18 us
    all_to_all x2 -> x1, blocking collectives: 294 us -> 191 us  [body(): lax.all_to_all(outgoing, ('section', 'tensor'), split_axis=0, concat_axis...]
    unnamed x4 -> x0, local copies, waits for them, and re-layouts: 68.8 us -> none
    select_n x1 -> x0, local copies, waits for them, and re-layouts: 34.7 us -> none  [body(): outgoing = jnp.take(blocks, order, axis=0)]
    all_to_all x1 -> x0, local copies, waits for them, and re-layouts: 33.7 us -> none  [body(): lax.all_to_all(outgoing, 'tensor', split_axis=2, concat_axis=1, tiled=True)]
    pallas_call x0 -> x2, Pallas kernels: none -> 26.2 us  [the longest x1 13.7 us: unpack(): pl.pallas_call(kernel, grid=(count,), in_specs=[pl.BlockSpec((1, rows, wi...]
    broadcast_in_dim x1 -> x0, other arithmetic: 11.8 us -> none  [body(): return (restored[None], block_sums[None])]
    gather x1 -> x0, local copies, waits for them, and re-layouts: 8.32 us -> none  [body(): outgoing = jnp.take(blocks, order, axis=0)]
    select_n x3 -> x1, other arithmetic: 8.32 us -> 1.18 us  [body(): target = (mine + offsets[0]) % count]
where the time goes in v1:
time: 220 us; the launch traced here: 219 us
  blocking collectives  191 us (87%)
  Pallas kernels  26.2 us (12%)
    all_to_all x1, blocking collectives, body(): lax.all_to_all(outgoing, ('section', 'tensor'), split_axis=0, concat_axis...  191 us
    pallas_call x1, Pallas kernels, unpack(): pl.pallas_call(kernel, grid=(count,), in_specs=[pl.BlockSpec((1, rows, wi...  13.7 us
    pallas_call x1, Pallas kernels, pack(): pl.pallas_call(kernel, grid_spec=pltpu.PrefetchScalarGridSpec(num_scalar_...  12.5 us

profile of v1, /device:TPU:1, one launch (start us, length us, event | category | flops | bytes accessed | tf_op | source)
XLA Modules:
  0.0 218.7 jit_solution(9698666347423879187)
XLA Ops:
  0.6 1.2 and_select_fusion.target_ref
  1.8 12.5 %pack.1 = bf16[16,2,32,4096]{3,2,1,0:T(8,128)(2,1)} custom-call(s32[16]{0:T(128)} %and_select_fusion.target_ref, bf16[16,32,8192]{2,1,0:T(8,128)(2,1)} %bitcast.7), custom_call_target="tpu_custom_call" | custom-call | tf_op jit(solution)/shard_map/pack/pallas_call | solution.py:17
  14.4 190.6 %all_to_all.5 = bf16[32,32,4096]{2,1,0:T(8,128)(2,1)} all-to-all(bf16[32,32,4096]{2,1,0:T(8,128)(2,1)} %bitcast.5), channel_id=1, replica_groups=mesh['section'=16,'tensor'=2] {'section','tensor'}, dimensions={0} | all-to-all | bytes 16777216 | tf_op jit(solution)/shard_map/all_to_all | solution.py:62
  205.0 13.7 %unpack.1 = (f32[1,16,64,4096]{3,2,1,0:T(8,128)}, f32[1,16,4096]{2,1,0:T(8,128)}) custom-call(bf16[16,64,4096]{2,1,0:T(8,128)(2,1)} %bitcast.6), custom_call_target="tpu_custom_call" | custom-call | tf_op jit(solution)/shard_map/unpack/pallas_call | solution.py:39
